TPU v7x, 32 devices: a whole 2x2x4 slice. The times are simulated.
32 devices in a mesh: mem: 8 (over y, x, core), patch: 4 (over z).
Axes of the slice: x: 2, y: 2, z: 4, core: 2. Of those that a mesh axis runs over, the one named last changes fastest.
Arguments:
- state: bfloat16 [1024, 16384], P('mem', 'patch'), may hold values from -6 to 6
- obs_ens: bfloat16 [1024, 8192], P('mem', 'patch'), may hold values from -6 to 6
- obs_values: float32 [8192], P('patch'), may hold values from -8 to 8
- obs_weight: float32 [8192], P('patch'), may hold values from 0.2 to 5
- counts: int32 [32], P('patch'), may hold values from 32 to 256
Outputs:
- analysis: bfloat16 [1024, 16384], P('mem', 'patch')
Inputs may be any that keep to these rules, and one draw needn't show every extreme that they name: Region r uses the first counts[r] of its 256 observations.
All inputs are finite; a program needn't handle non-finite values. Where the computation divides by a largest or mean magnitude, that divisor is 1e-20 or more.
Results may differ from a plain program's by a relative error of at most 0.0047.
Values may be sent and summed in bfloat16 or wider, within the bound.
A program may use at most 64 MiB of HBM per device.

v0:
```python
import functools
import math

import jax
import jax.numpy as jnp
import numpy as np
from jax import lax
from jax.experimental import pallas as pl
from jax.experimental.pallas import tpu as pltpu
from jax.sharding import PartitionSpec as P

DEGREE = 7
MESH = pl.DeviceIdType.MESH
PAD = 16


def functionals():
    number = DEGREE + 1
    theta = (np.arange(number) + 0.5) * (math.pi / number)
    rows = 2.0 / number * np.cos(np.arange(number)[:, None] * theta[None, :])
    rows[0] *= 0.5
    a = rows
    signs = np.where(np.arange(number) % 2 == 0, 1.0, -1.0)
    table = np.stack(
        [
            (signs[:, None] * a).sum(0),
            a[1] - a[7] + 2 * a[5],
            a[2] + a[6],
            a[3] - a[5] + 2 * a[7],
            a[4] - 2 * a[5] + 2 * a[6] - 2 * a[7],
            2 * a[5],
            2 * a[6],
            2 * a[7],
        ]
    )
    return (np.cos(theta) + 1.0) * 0.5, table


def flipped(index, step, count):
    bit = 1
    while bit < count:
        if step & bit:
            index = index + bit - 2 * bit * (lax.rem(index // bit, 2))
        bit *= 2
    return index


def split(row):
    high = row.astype(jnp.bfloat16)
    low = (row - high.astype(jnp.float32)).astype(jnp.bfloat16)
    return high, low


def row_times(row, matrix):
    high, low = split(row)
    k = row.shape[1]
    pick = lax.broadcasted_iota(jnp.int32, (PAD, k), 0)
    both = jnp.where(
        pick == 0,
        jnp.broadcast_to(high.astype(jnp.float32), (PAD, k)),
        jnp.where(pick == 1, jnp.broadcast_to(low.astype(jnp.float32), (PAD, k)), 0.0),
    ).astype(jnp.bfloat16)
    return jnp.sum(dot(both, matrix), axis=0, keepdims=True)


def dot(left, right):
    return jnp.dot(left, right, preferred_element_type=jnp.float32)


def kernel(
    n, npatch,
    val_hbm, wgt_hbm, cnt_hbm, obs_hbm, state_hbm, out_hbm,
    val_v, wgt_v, cnt_s, side, edge_v, obs_v, state_v, gain, gain_t, pt, out_v,
    d1, d2, d3, d4,
    obs_ss, obs_rs, st_ss, st_rs, edge_ss, edge_rs, side_ss, side_rs, out_ss, out_rs, loc,
):
    me = lax.axis_index("mem")
    patch = lax.axis_index("patch")
    rows = obs_hbm.shape[0]
    own = obs_v.shape[1]
    half = own // 2
    width = state_v.shape[1]
    members = n * rows
    nobs = 2 * own
    up = lax.rem(patch + 1, npatch)
    down = lax.rem(patch + npatch - 1, npatch)

    def cols(index, size):
        return pl.ds(pl.multiple_of(index * size, size), size)

    group = max(1, 256 // rows)
    groups = n // group
    order = list(range(groups - 1, 0, -1))
    steps = [s * group + i for i in range(group) for s in order[::-1]] + list(range(1, group))

    arrivals = list(range(1, group)) + [s for s in steps if s >= group]

    barrier = pltpu.get_barrier_semaphore()
    for s in range(1, n):
        pl.semaphore_signal(barrier, inc=1, device_id=(flipped(me, s, n), patch), device_id_type=MESH)
    for p in (up, down):
        pl.semaphore_signal(barrier, inc=1, device_id=(me, p), device_id_type=MESH)
    own_obs = pltpu.make_async_copy(obs_hbm.at[:, cols(me, own)], obs_v.at[cols(me, rows), :], loc.at[0])
    own_obs.start()
    own_state = pltpu.make_async_copy(state_hbm.at[:, cols(me, width)], state_v.at[cols(me, rows), :], loc.at[1])
    own_state.start()
    small = [
        pltpu.make_async_copy(src, dst, loc.at[3 + i])
        for i, (src, dst) in enumerate(((val_hbm, val_v), (wgt_hbm, wgt_v), (cnt_hbm, cnt_s)))
    ]
    for c in small:
        c.start()
    pl.semaphore_wait(barrier, n + 1)

    def obs_copy(s):
        peer = flipped(me, s, n)
        return pltpu.make_async_remote_copy(
            src_ref=obs_hbm.at[:, cols(peer, own)], dst_ref=obs_v.at[cols(me, rows), :],
            send_sem=obs_ss.at[s], recv_sem=obs_rs.at[s], device_id=(peer, patch), device_id_type=MESH)

    def state_copy(s):
        peer = flipped(me, s, n)
        return pltpu.make_async_remote_copy(
            src_ref=state_hbm.at[:, cols(peer, width)], dst_ref=state_v.at[cols(me, rows), :],
            send_sem=st_ss.at[s], recv_sem=st_rs.at[s], device_id=(peer, patch), device_id_type=MESH)

    def out_copy(s):
        peer = flipped(me, s, n)
        return pltpu.make_async_remote_copy(
            src_ref=out_v.at[cols(peer, rows), :], dst_ref=out_hbm.at[:, cols(me, width)],
            send_sem=out_ss.at[s], recv_sem=out_rs.at[s], device_id=(peer, patch), device_id_type=MESH)

    for s in steps:
        obs_copy(s).start()
    for s in steps:
        state_copy(s).start()

    def edge_copy(slot, s):
        block = cols(flipped(me, s, n), rows)
        return pltpu.make_async_remote_copy(
            src_ref=obs_v.at[block, pl.ds((1 - slot) * half, half)], dst_ref=edge_v.at[slot, block, :],
            send_sem=edge_ss.at[slot, s], recv_sem=edge_rs.at[slot, s],
            device_id=(me, down if slot else up), device_id_type=MESH)

    def side_copy(slot):
        return pltpu.make_async_remote_copy(
            src_ref=side.at[1 - slot], dst_ref=side.at[2 + slot],
            send_sem=side_ss.at[slot], recv_sem=side_rs.at[slot],
            device_id=(me, down if slot else up), device_id_type=MESH)

    own_obs.wait()
    for slot in range(2):
        edge_copy(slot, 0).start()
    for c in small:
        c.wait()
    count = cnt_s[me]
    for k in range(2):
        lane = lax.broadcasted_iota(jnp.int32, (1, half), 1) + k * half
        mask = jnp.where(lane < count, 1.0, 0.0)
        root = jnp.sqrt(wgt_v[pl.ds(2 * me + k, 1), :] * mask)
        pick = lax.broadcasted_iota(jnp.int32, (8, half), 0)
        side[k] = jnp.where(pick == 0, root, val_v[pl.ds(2 * me + k, 1), :])
    for s in arrivals:
        obs_copy(s).wait_recv()
        for slot in range(2):
            edge_copy(slot, s).start()
    for slot in range(2):
        side_copy(slot).start()

    innovs = [None] * 4

    def perturb(k, block):
        full = block.astype(jnp.float32)
        centre = jnp.sum(full, axis=0, keepdims=True) * (1.0 / members)
        root = side[k, pl.ds(0, 1), :]
        values = side[k, pl.ds(1, 1), :]
        scaled_block = ((full - centre) * root).astype(jnp.bfloat16)
        gain[k] = scaled_block
        gain_t[pl.ds(k * half, half), :] = scaled_block.T
        innovs[k] = (root * (values - centre)).astype(jnp.bfloat16).astype(jnp.float32)

    for k in range(2):
        perturb(k, obs_v[:, k * half:(k + 1) * half])
    for slot in range(2):
        side_copy(slot).wait_recv()
        for s in range(n):
            edge_copy(slot, s).wait_recv()
    for slot in range(2):
        perturb(2 + slot, edge_v[slot])

    def gains_of(r0, size):
        return jnp.concatenate([gain[k, pl.ds(r0, size), :] for k in range(4)], axis=1)

    normal = dot(gain_t[...], gains_of(0, members))
    upper = jnp.max(jnp.sum(jnp.abs(normal), axis=0, keepdims=True), axis=1, keepdims=True)
    upper = upper * (1.0 / (members - 1)) + 1e-06
    scaled = normal * (2.0 / (members - 1) / upper)
    d1[...] = scaled.astype(jnp.bfloat16)

    nodes, table = functionals()
    wide = jnp.broadcast_to(upper, (1, nobs))
    f_samples, e_samples = [], []
    for k in range(DEGREE + 1):
        m = wide * float(nodes[k])
        lifted = jnp.sqrt(1.0 + m)
        f_samples.append(-1.0 / (lifted * (1.0 + lifted)))
        e_samples.append(1.0 / (1.0 + m))

    def combined(samples):
        out = []
        for j in range(DEGREE + 1):
            total = samples[0] * float(table[j, 0])
            for k in range(1, DEGREE + 1):
                total = total + samples[k] * float(table[j, k])
            out.append(total)
        return out

    fa = combined(f_samples)
    ea = combined(e_samples)

    t = scaled
    second = 2.0 * dot(d1[...], d1[...]) - 4.0 * t
    d2[...] = second.astype(jnp.bfloat16)
    third = 2.0 * dot(d1[...], d2[...]) + t - 2.0 * second
    d3[...] = third.astype(jnp.bfloat16)
    fourth = 2.0 * dot(d2[...], d2[...]) + 4.0 * second
    d4[...] = fourth.astype(jnp.bfloat16)
    tail = fa[5] * t + fa[6] * second + fa[7] * third
    poly = fa[1] * t + fa[2] * second + fa[3] * third + fa[4] * fourth + dot(d4[...], tail.astype(jnp.bfloat16))

    dvec = jnp.concatenate(innovs, axis=1)
    y1 = row_times(dvec, d1[...])
    y2 = row_times(dvec, d2[...])
    y3 = row_times(dvec, d3[...])
    w = ea[5] * y1 + ea[6] * y2 + ea[7] * y3
    y4 = row_times(w + ea[4] * dvec, d4[...])
    u = ea[0] * dvec + ea[1] * y1 + ea[2] * y2 + ea[3] * y3 + y4
    poly_b = poly.astype(jnp.bfloat16)

    gsum = jnp.sum(gain_t[...].astype(jnp.float32), axis=1, keepdims=True)
    csum = jnp.zeros((1, width), jnp.float32)
    gr = group * rows
    for i, s in enumerate([0] + order[::-1]):
        base = flipped(me // group, s, groups)
        if s == 0:
            own_state.wait()
        for j in range(group):
            if s * group + j:
                state_copy(s * group + j).wait_recv()
        block = state_v[cols(base, gr), :]
        csum = csum + jnp.sum(block.astype(jnp.float32), axis=0, keepdims=True)
        part = dot(gain_t[:, cols(base, gr)], block)
        if i == 0:
            pt[...] = part
        else:
            pt[...] += part
    product = pt[...] - gsum * (csum * (1.0 / members))
    product_b = product.astype(jnp.bfloat16)
    scale = 1.0 / (members - 1)
    mixed = (fa[0][:, 0:1] * product + dot(poly_b, product_b)) * scale
    d1[...] = mixed.astype(jnp.bfloat16)
    shift = row_times(u, product_b) * scale

    for s in order + [0]:
        base = flipped(me // group, s, groups)
        start = pl.multiple_of(base * gr, gr)
        g = jnp.concatenate([gain[k, pl.ds(start, gr), :] for k in range(4)], axis=1)
        update = dot(g, d1[...])
        out_v[cols(base, gr), :] = (
            state_v[cols(base, gr), :].astype(jnp.float32) + shift + update
        ).astype(jnp.bfloat16)
        for j in range(group):
            if s * group + j:
                out_copy(s * group + j).start()
    keep = pltpu.make_async_copy(out_v.at[cols(me, rows), :], out_hbm.at[:, cols(me, width)], loc.at[2])
    keep.start()

    for slot in range(2):
        side_copy(slot).wait_send()
        for s in range(n):
            edge_copy(slot, s).wait_send()
    for s in range(1, n):
        obs_copy(s).wait_send()
        state_copy(s).wait_send()
    keep.wait()
    for s in range(1, n):
        out_copy(s).wait()


def on_device(n, npatch, state, obs_ens, obs_values, obs_weight, counts):
    rows = obs_ens.shape[0]
    own = obs_ens.shape[1] // n
    width = state.shape[1] // n
    members = rows * n
    nobs = 2 * own
    half = own // 2
    bf, f32 = jnp.bfloat16, jnp.float32
    dma = pltpu.SemaphoreType.DMA
    hbm = pl.BlockSpec(memory_space=pl.ANY)
    return pl.pallas_call(
        functools.partial(kernel, n, npatch),
        out_shape=jax.ShapeDtypeStruct(state.shape, bf),
        in_specs=[pl.BlockSpec(memory_space=pltpu.HBM)] * 5,
        out_specs=hbm,
        scratch_shapes=[
            pltpu.VMEM((2 * n, half), f32),
            pltpu.VMEM((2 * n, half), f32),
            pltpu.SMEM((n,), jnp.int32),
            pltpu.VMEM((4, 8, half), f32),
            pltpu.VMEM((2, members, half), bf),
            pltpu.VMEM((members, own), bf),
            pltpu.VMEM((members, width), bf),
            pltpu.VMEM((4, members, half), bf),
            pltpu.VMEM((nobs, members), bf),
            pltpu.VMEM((nobs, width), f32),
            pltpu.VMEM((members, width), bf),
            pltpu.VMEM((nobs, nobs), bf),
            pltpu.VMEM((nobs, nobs), bf),
            pltpu.VMEM((nobs, nobs), bf),
            pltpu.VMEM((nobs, nobs), bf),
            dma((n,)), dma((n,)), dma((n,)), dma((n,)),
            dma((2, n)), dma((2, n)), dma((2,)), dma((2,)), dma((n,)), dma((n,)), dma((6,)),
        ],
        compiler_params=pltpu.CompilerParams(collective_id=0, has_side_effects=True, vmem_limit_bytes=28 * 1024 * 1024),
    )(*(pltpu.with_memory_space_constraint(x, pltpu.HBM) for x in (obs_values.reshape(2 * n, half), obs_weight.reshape(2 * n, half), counts, obs_ens, state)))


def solution(mesh):
    placed = (P("mem", "patch"), P("mem", "patch"), P("patch"), P("patch"), P("patch"))
    body = functools.partial(on_device, mesh.shape["mem"], mesh.shape["patch"])
    return jax.shard_map(
        body, mesh=mesh, in_specs=placed, out_specs=P("mem", "patch"), check_vma=False
    )
```

profile of v0, /device:TPU:1, one launch (start us, length us, event | category | flops | bytes accessed | tf_op | source)
XLA Modules:
  0.0 39.7 jit_solution(13643870327065066406)
XLA Ops:
  0.0 38.7 %shard_map.55 = bf16[128,4096]{1,0:T(8,128)(2,1)S(1)} custom-call(f32[16,128]{1,0:T(8,128)} %bitcast.2, f32[16,128]{1,0:T(8,128)} %bitcast.3, s32[8]{0:T(128)} %cnt_hbm.1, bf16[128,2048]{1,0:T(8,128)(2,1)} %obs_hbm.1, bf16[128,4096]{1,0:T(8,128)(2,1)} %state_hbm.1), custom_call_target="tpu_custom_call" | custom-call | tf_op jit(solution)/shard_map/pallas_call | solution.py:300
  38.7 1.0 %copy.7 = bf16[128,4096]{1,0:T(8,128)(2,1)} copy(bf16[128,4096]{1,0:T(8,128)(2,1)S(1)} %shard_map.55) | data formatting | bytes 2097152
where the time goes:
time: 40.2 us; the launch traced here: 39.7 us
  Pallas kernels  38.7 us (96%)
  local copies, waits for them, and re-layouts  0.97 us (2%)
    pallas_call x1, Pallas kernels, on_device(): pl.pallas_call(functools.partial(kernel, n, npatch), out_shape=jax.ShapeD...  38.7 us
    unnamed x1, local copies, waits for them, and re-layouts  0.97 us

commit v1 on v0

v1 whole, which is shorter than its diff:
```python
import functools
import math

import jax
import jax.numpy as jnp
import numpy as np
from jax import lax
from jax.experimental import pallas as pl
from jax.experimental.pallas import tpu as pltpu
from jax.sharding import PartitionSpec as P

DEGREE = 7
MESH = pl.DeviceIdType.MESH
PAD = 16
CHUNKS = 2


def functionals():
    number = DEGREE + 1
    theta = (np.arange(number) + 0.5) * (math.pi / number)
    rows = 2.0 / number * np.cos(np.arange(number)[:, None] * theta[None, :])
    rows[0] *= 0.5
    a = rows
    signs = np.where(np.arange(number) % 2 == 0, 1.0, -1.0)
    table = np.stack(
        [
            (signs[:, None] * a).sum(0),
            a[1] - a[7] + 2 * a[5],
            a[2] + a[6],
            a[3] - a[5] + 2 * a[7],
            a[4] - 2 * a[5] + 2 * a[6] - 2 * a[7],
            2 * a[5],
            2 * a[6],
            2 * a[7],
        ]
    )
    return (np.cos(theta) + 1.0) * 0.5, table


def flipped(index, step, count):
    bit = 1
    while bit < count:
        if step & bit:
            index = index + bit - 2 * bit * (lax.rem(index // bit, 2))
        bit *= 2
    return index


def dot(left, right):
    return jnp.dot(left, right, preferred_element_type=jnp.float32)


def pair_rows(row):
    high = row.astype(jnp.bfloat16).astype(jnp.float32)
    k = row.shape[1]
    pick = lax.broadcasted_iota(jnp.int32, (PAD, k), 0)
    wide = (PAD, k)
    return jnp.where(
        pick == 0,
        jnp.broadcast_to(high, wide),
        jnp.where(pick == 1, jnp.broadcast_to(row - high, wide), 0.0),
    ).astype(jnp.bfloat16)


def rows_sum(block):
    return jnp.sum(block, axis=0, keepdims=True)


def kernel(
    n, npatch,
    val_hbm, wgt_hbm, cnt_hbm, obs_hbm, state_hbm, out_hbm,
    val_v, wgt_v, cnt_s, side, obs_s, state_s, edge_v, obs_v, state_v, gain, gain_t, acc, pt, out_v,
    d1, d2, d4, px, mix,
    obs_ss, obs_rs, st_ss, st_rs, edge_ss, edge_rs, side_ss, side_rs, out_ss, out_rs, loc,
):
    me = lax.axis_index("mem")
    patch = lax.axis_index("patch")
    rows = obs_hbm.shape[0]
    own = obs_v.shape[1]
    half = own // 2
    width = state_v.shape[1]
    wc = width // CHUNKS
    members = n * rows
    nobs = 2 * own
    up = lax.rem(patch + 1, npatch)
    down = lax.rem(patch + npatch - 1, npatch)
    f32, bf = jnp.float32, jnp.bfloat16

    def cols(index, size):
        return pl.ds(pl.multiple_of(index * size, size), size)

    def part(index, c):
        return pl.ds(pl.multiple_of(index * width + c * wc, wc), wc)

    group = max(1, 256 // rows)
    groups = n // group
    gr = group * rows
    far = list(range(1, groups))
    near = list(range(1, group))
    steps = near + [s * group + i for i in range(group) for s in far]
    order = [0] + far

    barrier = pltpu.get_barrier_semaphore()
    for s in steps:
        pl.semaphore_signal(barrier, inc=1, device_id=(flipped(me, s, n), patch), device_id_type=MESH)
    for p in (up, down):
        pl.semaphore_signal(barrier, inc=1, device_id=(me, p), device_id_type=MESH)
    load_obs = pltpu.make_async_copy(obs_hbm, obs_s, loc.at[6])
    load_obs.start()
    own_obs = pltpu.make_async_copy(obs_hbm.at[:, cols(me, own)], obs_v.at[cols(me, rows), :], loc.at[0])
    own_obs.start()
    small = [
        pltpu.make_async_copy(src, dst, loc.at[3 + i])
        for i, (src, dst) in enumerate(((val_hbm, val_v), (wgt_hbm, wgt_v), (cnt_hbm, cnt_s)))
    ]
    for c in small:
        c.start()
    load_state = pltpu.make_async_copy(state_hbm, state_s, loc.at[7])
    load_state.start()
    own_state = pltpu.make_async_copy(state_hbm.at[:, cols(me, width)], state_v.at[cols(me, rows), :], loc.at[1])
    own_state.start()

    def obs_copy(s):
        peer = flipped(me, s, n)
        return pltpu.make_async_remote_copy(
            src_ref=obs_s.at[:, cols(peer, own)], dst_ref=obs_v.at[cols(me, rows), :],
            send_sem=obs_ss.at[s], recv_sem=obs_rs.at[s], device_id=(peer, patch), device_id_type=MESH)

    def state_copy(s, c):
        peer = flipped(me, s, n)
        return pltpu.make_async_remote_copy(
            src_ref=state_s.at[:, part(peer, c)], dst_ref=state_v.at[cols(me, rows), pl.ds(c * wc, wc)],
            send_sem=st_ss.at[c, s], recv_sem=st_rs.at[c, s], device_id=(peer, patch), device_id_type=MESH)

    def out_copy(s, c):
        peer = flipped(me, s, n)
        return pltpu.make_async_remote_copy(
            src_ref=out_v.at[cols(peer, rows), pl.ds(c * wc, wc)], dst_ref=out_hbm.at[:, part(me, c)],
            send_sem=out_ss.at[c, s], recv_sem=out_rs.at[c, s], device_id=(peer, patch), device_id_type=MESH)

    def edge_copy(slot, s):
        block = cols(flipped(me, s, n), rows)
        return pltpu.make_async_remote_copy(
            src_ref=obs_v.at[block, pl.ds((1 - slot) * half, half)], dst_ref=edge_v.at[slot, block, :],
            send_sem=edge_ss.at[slot, s], recv_sem=edge_rs.at[slot, s],
            device_id=(me, down if slot else up), device_id_type=MESH)

    def side_copy(slot):
        return pltpu.make_async_remote_copy(
            src_ref=side.at[1 - slot], dst_ref=side.at[2 + slot],
            send_sem=side_ss.at[slot], recv_sem=side_rs.at[slot],
            device_id=(me, down if slot else up), device_id_type=MESH)

    load_obs.wait()
    own_obs.wait()
    pl.semaphore_wait(barrier, n + 1)
    for s in near:
        obs_copy(s).start()
    for slot in range(2):
        edge_copy(slot, 0).start()
    for s in steps:
        if s >= group:
            obs_copy(s).start()
    load_state.wait()
    for c in range(CHUNKS):
        for s in steps:
            state_copy(s, c).start()

    for c in small:
        c.wait()
    count = cnt_s[me]
    roots = []
    for k in range(2):
        lane = lax.broadcasted_iota(jnp.int32, (1, half), 1) + k * half
        mask = jnp.where(lane < count, 1.0, 0.0)
        roots.append(jnp.sqrt(wgt_v[pl.ds(2 * me + k, 1), :] * mask))

    for s in steps:
        obs_copy(s).wait_recv()
        for slot in range(2):
            edge_copy(slot, s).start()

    def perturb(k, block, at, centre, root):
        scaled_block = ((block.astype(f32) - centre) * root).astype(bf)
        gain[k, at, :] = scaled_block
        gain_t[pl.ds(k * half, half), at] = scaled_block.T

    innovs = [None] * 4

    def innov(k, centre, root, values):
        innovs[k] = (root * (values - centre)).astype(bf).astype(f32)

    for k in range(2):
        block = obs_v[:, k * half:(k + 1) * half]
        centre = rows_sum(block.astype(f32)) * (1.0 / members)
        values = val_v[pl.ds(2 * me + k, 1), :]
        pick = lax.broadcasted_iota(jnp.int32, (8, half), 0)
        side[k] = jnp.where(pick == 0, roots[k], jnp.where(pick == 1, values, centre))
        innov(k, centre, roots[k], values)
        perturb(k, block, pl.ds(0, members), centre, roots[k])
    for slot in range(2):
        side_copy(slot).start()
    for slot in range(2):
        side_copy(slot).wait_recv()
    edge_root, edge_centre = [], []
    for slot in range(2):
        root, values, centre = (side[2 + slot, pl.ds(i, 1), :] for i in range(3))
        edge_root.append(root)
        edge_centre.append(centre)
        innov(2 + slot, centre, root, values)
    dvec = jnp.concatenate(innovs, axis=1)

    def gains_of(at):
        return jnp.concatenate([gain[k, at, :] for k in range(4)], axis=1)

    normal = None
    for i, s in enumerate(order):
        base = flipped(me // group, s, groups)
        at = cols(base, gr)
        for slot in range(2):
            for j in range(group):
                edge_copy(slot, s * group + j).wait_recv()
        for slot in range(2):
            perturb(2 + slot, edge_v[slot, at, :], at, edge_centre[slot], edge_root[slot])
        piece = dot(gain_t[:, at], gains_of(at))
        if i < groups - 1:
            acc[...] = piece if i == 0 else acc[...] + piece
        else:
            normal = piece if i == 0 else acc[...] + piece

    upper = jnp.max(jnp.sum(jnp.abs(normal), axis=0, keepdims=True), axis=1, keepdims=True)
    upper = upper * (1.0 / (members - 1)) + 1e-06
    t = normal * (2.0 / (members - 1) / upper)
    d1[pl.ds(0, nobs), :] = t.astype(bf)
    d1[pl.ds(nobs, PAD), :] = pair_rows(dvec)

    nodes, table = functionals()
    wide = jnp.broadcast_to(upper, (1, nobs))
    f_samples, e_samples = [], []
    for k in range(DEGREE + 1):
        m = wide * float(nodes[k])
        lifted = jnp.sqrt(1.0 + m)
        f_samples.append(-1.0 / (lifted * (1.0 + lifted)))
        e_samples.append(1.0 / (1.0 + m))

    def combined(samples):
        out = []
        for j in range(DEGREE + 1):
            total = samples[0] * float(table[j, 0])
            for k in range(1, DEGREE + 1):
                total = total + samples[k] * float(table[j, k])
            out.append(total)
        return out

    fa = combined(f_samples)
    ea = combined(e_samples)
    top, extra = pl.ds(0, nobs), pl.ds(nobs, PAD)

    r1 = d1[top, :]
    prod = dot(d1[...], r1)
    second = 2.0 * prod[:nobs] - 4.0 * t
    y1 = rows_sum(prod[nobs:])
    d2[top, :] = second.astype(bf)
    d2[extra, :] = pair_rows(y1)
    r2 = d2[top, :]
    prod3 = dot(d1[...], r2)
    prod4 = dot(d2[...], r2)
    third = 2.0 * prod3[:nobs] + t - 2.0 * second
    fourth = 2.0 * prod4[:nobs] + 4.0 * second
    d4[...] = fourth.astype(bf)
    y2 = rows_sum(prod3[nobs:])
    y3 = 2.0 * rows_sum(prod4[nobs:]) + y1 - 2.0 * y2
    px[top, :] = (fa[5] * t + fa[6] * second + fa[7] * third).astype(bf)
    px[extra, :] = pair_rows(ea[5] * y1 + ea[6] * y2 + ea[7] * y3 + ea[4] * dvec)
    low = fa[1] * t + fa[2] * second + fa[3] * third + fa[4] * fourth
    prod7 = dot(px[...], d4[...])
    poly = low + prod7[:nobs]
    u = ea[0] * dvec + ea[1] * y1 + ea[2] * y2 + ea[3] * y3 + rows_sum(prod7[nobs:])
    px[top, :] = poly.astype(bf)
    px[extra, :] = pair_rows(u)

    gsum = jnp.sum(gain_t[...].astype(f32), axis=1, keepdims=True)
    scale = 1.0 / (members - 1)
    fa0 = fa[0][:, 0:1]

    for c in range(CHUNKS):
        here = pl.ds(c * wc, wc)
        csum = jnp.zeros((1, wc), f32)
        if c == 0:
            own_state.wait()
        for i, s in enumerate(order):
            base = flipped(me // group, s, groups)
            for j in range(group):
                if s * group + j:
                    state_copy(s * group + j, c).wait_recv()
            block = state_v[cols(base, gr), here]
            csum = csum + rows_sum(block.astype(f32))
            piece = dot(gain_t[:, cols(base, gr)], block)
            pt[...] = piece if i == 0 else pt[...] + piece
        product = pt[...] - gsum * (csum * (1.0 / members))
        product_b = product.astype(bf)
        both = dot(px[...], product_b)
        mix[...] = ((fa0 * product + both[:nobs]) * scale).astype(bf)
        shift = rows_sum(both[nobs:]) * scale
        for s in far + [0]:
            base = flipped(me // group, s, groups)
            at = cols(base, gr)
            update = dot(gains_of(at), mix[...])
            out_v[at, here] = (state_v[at, here].astype(f32) + shift + update).astype(bf)
            for j in range(group):
                if s * group + j:
                    out_copy(s * group + j, c).start()
    keep = pltpu.make_async_copy(out_v.at[cols(me, rows), :], out_hbm.at[:, cols(me, width)], loc.at[2])
    keep.start()

    for slot in range(2):
        side_copy(slot).wait_send()
        for s in range(n):
            edge_copy(slot, s).wait_send()
    for s in steps:
        obs_copy(s).wait_send()
        for c in range(CHUNKS):
            state_copy(s, c).wait_send()
    keep.wait()
    for c in range(CHUNKS):
        for s in steps:
            out_copy(s, c).wait()


def on_device(n, npatch, state, obs_ens, obs_values, obs_weight, counts):
    rows = obs_ens.shape[0]
    own = obs_ens.shape[1] // n
    width = state.shape[1] // n
    members = rows * n
    nobs = 2 * own
    half = own // 2
    wc = width // CHUNKS
    bf, f32 = jnp.bfloat16, jnp.float32
    dma = pltpu.SemaphoreType.DMA
    hbm = pl.BlockSpec(memory_space=pl.ANY)
    return pl.pallas_call(
        functools.partial(kernel, n, npatch),
        out_shape=jax.ShapeDtypeStruct(state.shape, bf),
        in_specs=[pl.BlockSpec(memory_space=pltpu.HBM)] * 5,
        out_specs=hbm,
        scratch_shapes=[
            pltpu.VMEM((2 * n, half), f32),
            pltpu.VMEM((2 * n, half), f32),
            pltpu.SMEM((n,), jnp.int32),
            pltpu.VMEM((4, 8, half), f32),
            pltpu.VMEM(obs_ens.shape, bf),
            pltpu.VMEM(state.shape, bf),
            pltpu.VMEM((2, members, half), bf),
            pltpu.VMEM((members, own), bf),
            pltpu.VMEM((members, width), bf),
            pltpu.VMEM((4, members, half), bf),
            pltpu.VMEM((nobs, members), bf),
            pltpu.VMEM((nobs, nobs), f32),
            pltpu.VMEM((nobs, wc), f32),
            pltpu.VMEM((members, width), bf),
            pltpu.VMEM((nobs + PAD, nobs), bf),
            pltpu.VMEM((nobs + PAD, nobs), bf),
            pltpu.VMEM((nobs, nobs), bf),
            pltpu.VMEM((nobs + PAD, nobs), bf),
            pltpu.VMEM((nobs, wc), bf),
            dma((n,)), dma((n,)), dma((CHUNKS, n)), dma((CHUNKS, n)),
            dma((2, n)), dma((2, n)), dma((2,)), dma((2,)), dma((CHUNKS, n)), dma((CHUNKS, n)), dma((8,)),
        ],
        compiler_params=pltpu.CompilerParams(collective_id=0, has_side_effects=True, vmem_limit_bytes=28 * 1024 * 1024),
    )(*(pltpu.with_memory_space_constraint(x, pltpu.HBM) for x in (obs_values.reshape(2 * n, half), obs_weight.reshape(2 * n, half), counts, obs_ens, state)))


def solution(mesh):
    placed = (P("mem", "patch"), P("mem", "patch"), P("patch"), P("patch"), P("patch"))
    body = functools.partial(on_device, mesh.shape["mem"], mesh.shape["patch"])
    return jax.shard_map(
        body, mesh=mesh, in_specs=placed, out_specs=P("mem", "patch"), check_vma=False
    )
```

time: 40.2 us -> 38.7 us (0.963)
  Pallas kernels: 38.7 us -> 37.6 us
    pallas_call x1, Pallas kernels: 38.7 us -> 37.6 us  [on_device(): pl.pallas_call(functools.partial(kernel, n, npatch), out_shape=jax.ShapeD...]
where the time goes in v1:
time: 38.7 us; the launch traced here: 38.6 us
  Pallas kernels  37.6 us (97%)
  local copies, waits for them, and re-layouts  0.97 us (3%)
    pallas_call x1, Pallas kernels, on_device(): pl.pallas_call(functools.partial(kernel, n, npatch), out_shape=jax.ShapeD...  37.6 us
    unnamed x1, local copies, waits for them, and re-layouts  0.97 us

profile of v1, /device:TPU:1, one launch (start us, length us, event | category | flops | bytes accessed | tf_op | source)
XLA Modules:
  0.0 38.6 jit_solution(16914810708975541036)
XLA Ops:
  0.0 37.6 %shard_map.55 = bf16[128,4096]{1,0:T(8,128)(2,1)S(1)} custom-call(f32[16,128]{1,0:T(8,128)} %bitcast.2, f32[16,128]{1,0:T(8,128)} %bitcast.3, s32[8]{0:T(128)} %cnt_hbm.1, bf16[128,2048]{1,0:T(8,128)(2,1)} %obs_hbm.1, bf16[128,4096]{1,0:T(8,128)(2,1)} %state_hbm.1), custom_call_target="tpu_custom_call" | custom-call | tf_op jit(solution)/shard_map/pallas_call | solution.py:341
  37.6 1.0 %copy.7 = bf16[128,4096]{1,0:T(8,128)(2,1)} copy(bf16[128,4096]{1,0:T(8,128)(2,1)S(1)} %shard_map.55) | data formatting | bytes 2097152

commit v2 on v1

--- a/solution.py
+++ b/solution.py
@@ -96,6 +96,7 @@
     groups = n // group
     gr = group * rows
     far = list(range(1, groups))
+    mine = me // group
     near = list(range(1, group))
     steps = near + [s * group + i for i in range(group) for s in far]
     order = [0] + far
@@ -213,6 +214,19 @@
     def gains_of(at):
         return jnp.concatenate([gain[k, at, :] for k in range(4)], axis=1)
 
+    def add_group(c, i, total):
+        at = cols(flipped(mine, order[i], groups), gr)
+        block = state_v[at, pl.ds(c * wc, wc)]
+        piece = dot(gain_t[:, at], block)
+        pt[...] = piece if i == 0 else pt[...] + piece
+        return total + rows_sum(block.astype(f32))
+
+    def state_waits(c):
+        if c == 0:
+            own_state.wait()
+        for s in steps:
+            state_copy(s, c).wait_recv()
+
     normal = None
     for i, s in enumerate(order):
         base = flipped(me // group, s, groups)
@@ -228,12 +242,16 @@
         else:
             normal = piece if i == 0 else acc[...] + piece
 
+    csum = jnp.zeros((1, wc), f32)
+    state_waits(0)
     upper = jnp.max(jnp.sum(jnp.abs(normal), axis=0, keepdims=True), axis=1, keepdims=True)
     upper = upper * (1.0 / (members - 1)) + 1e-06
     t = normal * (2.0 / (members - 1) / upper)
     d1[pl.ds(0, nobs), :] = t.astype(bf)
     d1[pl.ds(nobs, PAD), :] = pair_rows(dvec)
 
+    for i in range(groups):
+        csum = add_group(0, i, csum)
     nodes, table = functionals()
     wide = jnp.broadcast_to(upper, (1, nobs))
     f_samples, e_samples = [], []
@@ -285,18 +303,11 @@
 
     for c in range(CHUNKS):
         here = pl.ds(c * wc, wc)
-        csum = jnp.zeros((1, wc), f32)
-        if c == 0:
-            own_state.wait()
-        for i, s in enumerate(order):
-            base = flipped(me // group, s, groups)
-            for j in range(group):
-                if s * group + j:
-                    state_copy(s * group + j, c).wait_recv()
-            block = state_v[cols(base, gr), here]
-            csum = csum + rows_sum(block.astype(f32))
-            piece = dot(gain_t[:, cols(base, gr)], block)
-            pt[...] = piece if i == 0 else pt[...] + piece
+        if c:
+            csum = jnp.zeros((1, wc), f32)
+            state_waits(c)
+            for i in range(groups):
+                csum = add_group(c, i, csum)
         product = pt[...] - gsum * (csum * (1.0 / members))
         product_b = product.astype(bf)
         both = dot(px[...], product_b)

time: 38.7 us -> 38 us (0.982)
  Pallas kernels: 37.6 us -> 36.8 us
    pallas_call x1, Pallas kernels: 37.6 us -> 36.8 us  [on_device(): pl.pallas_call(functools.partial(kernel, n, npatch), out_shape=jax.ShapeD...]
where the time goes in v2:
time: 38 us; the launch traced here: 37.8 us
  Pallas kernels  36.8 us (97%)
  local copies, waits for them, and re-layouts  0.97 us (3%)
    pallas_call x1, Pallas kernels, on_device(): pl.pallas_call(functools.partial(kernel, n, npatch), out_shape=jax.ShapeD...  36.8 us
    unnamed x1, local copies, waits for them, and re-layouts  0.97 us

profile of v2, /device:TPU:1, one launch (start us, length us, event | category | flops | bytes accessed | tf_op | source)
XLA Modules:
  0.0 37.8 jit_solution(10801098863468866504)
XLA Ops:
  0.0 36.8 %shard_map.55 = bf16[128,4096]{1,0:T(8,128)(2,1)S(1)} custom-call(f32[16,128]{1,0:T(8,128)} %bitcast.2, f32[16,128]{1,0:T(8,128)} %bitcast.3, s32[8]{0:T(128)} %cnt_hbm.1, bf16[128,2048]{1,0:T(8,128)(2,1)} %obs_hbm.1, bf16[128,4096]{1,0:T(8,128)(2,1)} %state_hbm.1), custom_call_target="tpu_custom_call" | custom-call | tf_op jit(solution)/shard_map/pallas_call | solution.py:352
  36.8 1.0 %copy.7 = bf16[128,4096]{1,0:T(8,128)(2,1)} copy(bf16[128,4096]{1,0:T(8,128)(2,1)S(1)} %shard_map.55) | data formatting | bytes 2097152

commit v3 on v2

--- a/solution.py
+++ b/solution.py
@@ -50,7 +50,7 @@
     return jnp.dot(left, right, preferred_element_type=jnp.float32)
 
 
-def pair_rows(row):
+def pair_rows(row, third=None):
     high = row.astype(jnp.bfloat16).astype(jnp.float32)
     k = row.shape[1]
     pick = lax.broadcasted_iota(jnp.int32, (PAD, k), 0)
@@ -58,7 +58,11 @@
     return jnp.where(
         pick == 0,
         jnp.broadcast_to(high, wide),
-        jnp.where(pick == 1, jnp.broadcast_to(row - high, wide), 0.0),
+        jnp.where(
+            pick == 1,
+            jnp.broadcast_to(row - high, wide),
+            0.0 if third is None else jnp.where(pick == 2, jnp.broadcast_to(third, wide), 0.0),
+        ),
     ).astype(jnp.bfloat16)
 
 
@@ -69,8 +73,8 @@
 def kernel(
     n, npatch,
     val_hbm, wgt_hbm, cnt_hbm, obs_hbm, state_hbm, out_hbm,
-    val_v, wgt_v, cnt_s, side, obs_s, state_s, edge_v, obs_v, state_v, gain, gain_t, acc, pt, out_v,
-    d1, d2, d4, px, mix,
+    val_v, wgt_v, cnt_s, side, obs_s, state_s, edge_v, obs_v, state_v, gain, gain_t, acc, out_v,
+    d1, d2, d4, mix,
     obs_ss, obs_rs, st_ss, st_rs, edge_ss, edge_rs, side_ss, side_rs, out_ss, out_rs, loc,
 ):
     me = lax.axis_index("mem")
@@ -178,7 +182,7 @@
 
     for s in steps:
         obs_copy(s).wait_recv()
-        for slot in range(2):
+        for slot in (1, 0):
             edge_copy(slot, s).start()
 
     def perturb(k, block, at, centre, root):
@@ -213,13 +217,6 @@
 
     def gains_of(at):
         return jnp.concatenate([gain[k, at, :] for k in range(4)], axis=1)
-
-    def add_group(c, i, total):
-        at = cols(flipped(mine, order[i], groups), gr)
-        block = state_v[at, pl.ds(c * wc, wc)]
-        piece = dot(gain_t[:, at], block)
-        pt[...] = piece if i == 0 else pt[...] + piece
-        return total + rows_sum(block.astype(f32))
 
     def state_waits(c):
         if c == 0:
@@ -242,7 +239,6 @@
         else:
             normal = piece if i == 0 else acc[...] + piece
 
-    csum = jnp.zeros((1, wc), f32)
     state_waits(0)
     upper = jnp.max(jnp.sum(jnp.abs(normal), axis=0, keepdims=True), axis=1, keepdims=True)
     upper = upper * (1.0 / (members - 1)) + 1e-06
@@ -250,8 +246,14 @@
     d1[pl.ds(0, nobs), :] = t.astype(bf)
     d1[pl.ds(nobs, PAD), :] = pair_rows(dvec)
 
-    for i in range(groups):
-        csum = add_group(0, i, csum)
+    gsum = jnp.sum(gain_t[...].astype(f32), axis=1, keepdims=True)
+
+    def product_of(c):
+        block = state_v[:, c * wc:(c + 1) * wc]
+        csum = rows_sum(block.astype(f32))
+        return dot(gain_t[...], block) - gsum * (csum * (1.0 / members))
+
+    product = product_of(0)
     nodes, table = functionals()
     wide = jnp.broadcast_to(upper, (1, nobs))
     f_samples, e_samples = [], []
@@ -273,54 +275,52 @@
     fa = combined(f_samples)
     ea = combined(e_samples)
     top, extra = pl.ds(0, nobs), pl.ds(nobs, PAD)
+    scale = 1.0 / (members - 1)
+    fc = [coef[:, :1] for coef in fa]
 
     r1 = d1[top, :]
-    prod = dot(d1[...], r1)
-    second = 2.0 * prod[:nobs] - 4.0 * t
-    y1 = rows_sum(prod[nobs:])
+    p0 = product.astype(bf)
+    squared = dot(d1[...], r1)
+    tp = dot(r1, p0)
+    second = 2.0 * squared[:nobs] - 4.0 * t
+    y1 = rows_sum(squared[nobs:])
     d2[top, :] = second.astype(bf)
-    d2[extra, :] = pair_rows(y1)
+    d2[extra, :] = pair_rows(y1, dvec)
     r2 = d2[top, :]
-    prod3 = dot(d1[...], r2)
-    prod4 = dot(d2[...], r2)
-    third = 2.0 * prod3[:nobs] + t - 2.0 * second
-    fourth = 2.0 * prod4[:nobs] + 4.0 * second
-    d4[...] = fourth.astype(bf)
-    y2 = rows_sum(prod3[nobs:])
-    y3 = 2.0 * rows_sum(prod4[nobs:]) + y1 - 2.0 * y2
-    px[top, :] = (fa[5] * t + fa[6] * second + fa[7] * third).astype(bf)
-    px[extra, :] = pair_rows(ea[5] * y1 + ea[6] * y2 + ea[7] * y3 + ea[4] * dvec)
-    low = fa[1] * t + fa[2] * second + fa[3] * third + fa[4] * fourth
-    prod7 = dot(px[...], d4[...])
-    poly = low + prod7[:nobs]
-    u = ea[0] * dvec + ea[1] * y1 + ea[2] * y2 + ea[3] * y3 + rows_sum(prod7[nobs:])
-    px[top, :] = poly.astype(bf)
-    px[extra, :] = pair_rows(u)
-
-    gsum = jnp.sum(gain_t[...].astype(f32), axis=1, keepdims=True)
-    scale = 1.0 / (members - 1)
-    fa0 = fa[0][:, 0:1]
-
-    for c in range(CHUNKS):
+    tp0 = tp.astype(bf)
+    fourth = dot(d2[...], r2)
+    sp = dot(r2, p0)
+    stp = dot(r2, tp0)
+    y2 = fourth[nobs + 2:nobs + 3]
+    y3 = 2.0 * (fourth[nobs:nobs + 1] + fourth[nobs + 1:nobs + 2]) + y1 - 2.0 * y2
+    d4[...] = (2.0 * fourth[:nobs] + 4.0 * second).astype(bf)
+    last = pair_rows(ea[4] * dvec + ea[5] * y1 + ea[6] * y2 + ea[7] * y3)
+    tail = rows_sum(dot(last, d4[...]))
+    u = pair_rows(ea[0] * dvec + ea[1] * y1 + ea[2] * y2 + ea[3] * y3 + tail)
+
+    def finish(product, tp, sp, stp, c):
         here = pl.ds(c * wc, wc)
-        if c:
-            csum = jnp.zeros((1, wc), f32)
-            state_waits(c)
-            for i in range(groups):
-                csum = add_group(c, i, csum)
-        product = pt[...] - gsum * (csum * (1.0 / members))
-        product_b = product.astype(bf)
-        both = dot(px[...], product_b)
-        mix[...] = ((fa0 * product + both[:nobs]) * scale).astype(bf)
-        shift = rows_sum(both[nobs:]) * scale
+        thirdp = 2.0 * stp + tp - 2.0 * sp
+        q = fc[4] * product + fc[5] * tp + fc[6] * sp + fc[7] * thirdp
+        low = fc[0] * product + fc[1] * tp + fc[2] * sp + fc[3] * thirdp
+        mix[...] = ((low + dot(d4[...], q.astype(bf))) * scale).astype(bf)
+        shift = rows_sum(dot(u, product.astype(bf))) * scale
         for s in far + [0]:
-            base = flipped(me // group, s, groups)
+            base = flipped(mine, s, groups)
             at = cols(base, gr)
             update = dot(gains_of(at), mix[...])
             out_v[at, here] = (state_v[at, here].astype(f32) + shift + update).astype(bf)
             for j in range(group):
                 if s * group + j:
                     out_copy(s * group + j, c).start()
+
+    finish(product, tp, sp, stp, 0)
+    for c in range(1, CHUNKS):
+        state_waits(c)
+        product = product_of(c)
+        p0 = product.astype(bf)
+        tp = dot(d1[top, :], p0)
+        finish(product, tp, dot(d2[top, :], p0), dot(d2[top, :], tp.astype(bf)), c)
     keep = pltpu.make_async_copy(out_v.at[cols(me, rows), :], out_hbm.at[:, cols(me, width)], loc.at[2])
     keep.start()
 
@@ -367,12 +367,10 @@
             pltpu.VMEM((4, members, half), bf),
             pltpu.VMEM((nobs, members), bf),
             pltpu.VMEM((nobs, nobs), f32),
-            pltpu.VMEM((nobs, wc), f32),
             pltpu.VMEM((members, width), bf),
             pltpu.VMEM((nobs + PAD, nobs), bf),
             pltpu.VMEM((nobs + PAD, nobs), bf),
             pltpu.VMEM((nobs, nobs), bf),
-            pltpu.VMEM((nobs + PAD, nobs), bf),
             pltpu.VMEM((nobs, wc), bf),
             dma((n,)), dma((n,)), dma((CHUNKS, n)), dma((CHUNKS, n)),
             dma((2, n)), dma((2, n)), dma((2,)), dma((2,)), dma((CHUNKS, n)), dma((CHUNKS, n)), dma((8,)),

time: 38 us -> 37.7 us (level)
  no operation moved by 1% of the time
where the time goes in v3:
time: 37.7 us; the launch traced here: 37.5 us
  Pallas kernels  36.5 us (97%)
  local copies, waits for them, and re-layouts  0.97 us (3%)
    pallas_call x1, Pallas kernels, on_device(): pl.pallas_call(functools.partial(kernel, n, npatch), out_shape=jax.ShapeD...  36.5 us
    unnamed x1, local copies, waits for them, and re-layouts  0.97 us

profile of v3, /device:TPU:1, one launch (start us, length us, event | category | flops | bytes accessed | tf_op | source)
XLA Modules:
  0.0 37.5 jit_solution(11831056882621411120)
XLA Ops:
  0.0 36.5 %shard_map.55 = bf16[128,4096]{1,0:T(8,128)(2,1)S(1)} custom-call(f32[16,128]{1,0:T(8,128)} %bitcast.2, f32[16,128]{1,0:T(8,128)} %bitcast.3, s32[8]{0:T(128)} %cnt_hbm.1, bf16[128,2048]{1,0:T(8,128)(2,1)} %obs_hbm.1, bf16[128,4096]{1,0:T(8,128)(2,1)} %state_hbm.1), custom_call_target="tpu_custom_call" | custom-call | tf_op jit(solution)/shard_map/pallas_call | solution.py:352
  36.6 1.0 %copy.7 = bf16[128,4096]{1,0:T(8,128)(2,1)} copy(bf16[128,4096]{1,0:T(8,128)(2,1)S(1)} %shard_map.55) | data formatting | bytes 2097152
